TPU v7x, 256 devices: a whole 4x4x8 slice. The times are simulated.
256 devices in a mesh: tok: 64 (over z, x, core), exp: 4 (over y).
Axes of the slice: x: 4, y: 4, z: 8, core: 2. Of those that a mesh axis runs over, the one named last changes fastest.
Arguments:
- tokens: bfloat16 [131072, 7168], P('tok', 'exp'), may hold values from -6 to 6
- gate_weight: bfloat16 [7168, 256], P('exp'), may hold values from -0.0625 to 0.0625
- expert_ids: int32 [131072, 8], P('tok'), may hold values from 0 to 255, all different within a row
- expert_bias: float32 [256], P('exp'), may hold values from -0.002 to 0.002
Outputs:
- affinities: float32 [131072, 256], P('tok', 'exp')
- weights: float32 [131072, 8], P('tok')
- load: float32 [256], replicated
- new_bias: float32 [256], replicated
All inputs are finite; a program needn't handle non-finite values.
Results may differ from a plain program's by a relative error of at most 0.0003.
Values may be sent and summed in bfloat16 or wider, within the bound.
A program may use at most 64 MiB of HBM per device.

v0:
```python
import jax
import jax.numpy as jnp
from jax import lax
from jax.sharding import Mesh
from jax.sharding import PartitionSpec as P

TOK = ("tok_0", "tok_1", "tok_2")


def split_up(shard, dim, length):
    shape = shard.shape
    pieces = shard.reshape(*shape[:dim], length, shape[dim] // length, *shape[dim + 1 :])
    return jnp.moveaxis(pieces, dim, 0)


def summed_on_arrival(shard, axis, dim):
    pieces = split_up(shard, dim, lax.axis_size(axis))
    arrived = lax.all_to_all(pieces, axis, split_axis=0, concat_axis=0, tiled=True)
    return arrived.sum(axis=0)


def copy_for_each(shard, axis):
    length = lax.axis_size(axis)
    return lax.all_to_all(
        jnp.broadcast_to(shard[None], (length, *shard.shape)), axis, 0, 0, tiled=True
    )


def taken_together(shard, axis):
    return copy_for_each(shard, axis).sum(axis=0)


def laid_out(pieces, dim):
    shape = list(pieces.shape[1:])
    shape[dim] *= pieces.shape[0]
    return jnp.moveaxis(pieces, 0, dim).reshape(shape)


def collect(shard, axis, dim):
    pieces = copy_for_each(shard, axis)
    return laid_out(pieces, dim)


def over_axes(shard, axes):
    for axis in axes:
        shard = lax.psum(shard, axis)
    return shard


def count_experts(expert_ids, width):
    numbers = lax.iota(jnp.int32, width)
    matches = expert_ids[:, :, None] == numbers[None, None, :]
    return jnp.sum(matches.astype(jnp.float32), axis=(0, 1))


def local(tokens, gate_weight, expert_ids, expert_bias):
    experts_all = gate_weight.shape[1]
    own_width = expert_bias.shape[0]
    first_expert = lax.axis_index("exp") * own_width
    tok_rows = tokens.shape[0]
    partial_logits = jnp.dot(tokens, gate_weight, preferred_element_type=jnp.float32)
    logits = summed_on_arrival(partial_logits, "exp", 1)
    affinities = jax.nn.sigmoid(logits)
    numbers = first_expert + lax.iota(jnp.int32, own_width)
    matches = expert_ids[:, :, None] == numbers[None, None, :]
    chosen_part = jnp.sum(jnp.where(matches, affinities[:, None, :], jnp.float32(0.0)), axis=2)
    chosen = taken_together(chosen_part, "exp")
    weights = 2.5 * chosen / jnp.sum(chosen, axis=1, keepdims=True)
    target = jnp.float32(tok_rows * lax.axis_size(TOK) * expert_ids.shape[1])
    bias_whole = collect(expert_bias, "exp", 0)
    load = over_axes(count_experts(expert_ids, experts_all), TOK)
    new_bias = bias_whole + 0.001 * jnp.sign(target - jnp.float32(experts_all) * load)
    return (affinities, weights, load, new_bias)


def solution(mesh):
    split = Mesh(
        mesh.devices.reshape(8, 4, 2, mesh.shape["exp"]), ("tok_0", "tok_1", "tok_2", "exp")
    )
    in_specs = (P(TOK, "exp"), P("exp", None), P(TOK, None), P("exp"))
    out_specs = (P(TOK, "exp"), P(TOK, None), P(), P())
    return jax.shard_map(local, mesh=split, in_specs=in_specs, out_specs=out_specs, check_vma=False)
```

profile of v0, /device:TPU:1, one launch (start us, length us, event | category | flops | bytes accessed | tf_op | source)
XLA Modules:
  0.0 75.2 jit_solution(5950804239624878363)
XLA Ops:
  0.6 0.0 copy-start
  0.6 1.3 %broadcast_in_dim.19 = f32[4,1,64]{2,1,0:T(1,128)} broadcast(f32[64]{0:T(128)} %param.7), dimensions={2} | broadcast | bytes 1280 | tf_op jit(solution)/shard_map/broadcast_in_dim | solution.py:25
  2.0 5.0 %all-to-all-start.2 = ((f32[4,1,64]{2,1,0:T(1,128)}), f32[4,1,64]{2,1,0:T(1,128)S(1)}, u32[]{:S(2)}, u32[]{:S(2)}) async-start(f32[4,1,64]{2,1,0:T(1,128)} %broadcast_in_dim.19), calls=%async_computation.2 | async-start | bytes 4096 | tf_op jit(solution)/shard_map/all_to_all | solution.py:24
  7.0 6.5 %fusion.1 = f32[2048,256]{0,1:T(8,128)} fusion(bf16[2048,1792]{1,0:T(8,128)(2,1)} %param.4, bf16[1792,256]{1,0:T(8,128)(2,1)S(1)} %copy-done), kind=kOutput, calls=%fused_computation.8 | convolution fusion | flops 1879048192 | bytes 10354688 | tf_op jit(solution)/shard_map/dot_general | solution.py:61
  13.5 0.0 all-to-all-done.2
  13.5 4.4 %all-to-all-start = ((f32[4,2048,64]{1,2,0:T(8,128)}), f32[4,2048,64]{1,2,0:T(8,128)S(1)}, u32[]{:S(2)}, u32[]{:S(2)}) async-start(f32[4,2048,64]{1,2,0:T(8,128)} %bitcast.5), calls=%async_computation | async-start | bytes 4194304 | tf_op jit(solution)/shard_map/all_to_all | solution.py:18
  17.9 1.3 %copy.14 = s32[2048,8]{1,0:T(8,128)} copy(s32[2048,8]{0,1:T(8,128)S(1)} %copy-done.2) | data formatting | bytes 131072 | tf_op args[2]
  19.2 7.0 %convert_reduce_fusion = f32[256]{0:T(256)S(1)} fusion(s32[2048,8]{1,0:T(8,128)} %copy.14), kind=kLoop, calls=%fused_computation | loop fusion | flops 12582656 | bytes 66560 | tf_op jit(solution)/shard_map/reduce_sum | solution.py:53
  26.2 17.4 %psum.21 = f32[256]{0:T(256)S(1)} all-reduce(f32[256]{0:T(256)S(1)} %convert_reduce_fusion), channel_id=1, replica_groups=mesh['tok_0'=8,'tok_1'=4,'tok_2'=2,'exp'=4] {'tok_0'}, use_global_device_ids=true, to_apply=%region_5.6 | all-reduce | flops 256 | bytes 2048 | tf_op jit(solution)/shard_map/psum | solution.py:46
  43.6 8.5 %psum.22 = f32[256]{0:T(256)S(1)} all-reduce(f32[256]{0:T(256)S(1)} %psum.21), channel_id=1, replica_groups=mesh['tok_0'=8,'tok_1'=4,'tok_2'=2,'exp'=4] {'tok_1'}, use_global_device_ids=true, to_apply=%region_6.7 | all-reduce | flops 256 | bytes 2048 | tf_op jit(solution)/shard_map/psum | solution.py:46
  52.1 8.2 %psum.23 = f32[256]{0:T(256)S(1)} all-reduce(f32[256]{0:T(256)S(1)} %psum.22), channel_id=1, replica_groups=mesh['tok_0'=8,'tok_1'=4,'tok_2'=2,'exp'=4] {'tok_2'}, use_global_device_ids=true, to_apply=%region_7.8 | all-reduce | flops 256 | bytes 2048 | tf_op jit(solution)/shard_map/psum | solution.py:46
  60.3 0.5 broadcast.26
  60.8 0.7 reduce.4
  61.5 0.1 reshape.35
  61.6 0.0 all-to-all-done
  61.6 0.2 reduce_sum.45
  61.8 0.1 add_divide_fusion
  61.9 0.0 copy-start.1
  61.9 1.5 %select_reduce_fusion = f32[2048,8]{0,1:T(8,128)S(1)} fusion(f32[2048,64]{0,1:T(8,128)S(1)} %add_divide_fusion, s32[2048,8]{0,1:T(8,128)} %param.6, s32[64]{0:T(128)S(1)} %iota_add_fusion), kind=kLoop, calls=%fused_computation.2 | loop fusion | flops 3129344 | bytes 655616 | tf_op jit(solution)/shard_map/reduce_sum | solution.py:66
  63.4 0.7 broadcast_in_dim.18
  64.1 4.5 %all-to-all-start.1 = ((f32[4,2048,8]{1,2,0:T(8,128)}), f32[4,2048,8]{1,2,0:T(8,128)S(1)}, u32[]{:S(2)}, u32[]{:S(2)}) async-start(f32[4,2048,8]{1,2,0:T(8,128)} %broadcast_in_dim.18), calls=%async_computation.1 | async-start | bytes 524288 | tf_op jit(solution)/shard_map/all_to_all | solution.py:24
  68.6 0.6 multiply_add_fusion
  69.2 5.3 %all-to-all-done.1 = f32[4,2048,8]{1,2,0:T(8,128)S(1)} async-done(((f32[4,2048,8]{1,2,0:T(8,128)}), f32[4,2048,8]{1,2,0:T(8,128)S(1)}, u32[]{:S(2)}, u32[]{:S(2)}) %all-to-all-start.1) | async-done | bytes 262176 | tf_op jit(solution)/shard_map/all_to_all | solution.py:24
  74.5 0.6 multiply_divide_fusion
  (8 shorter events, 0.0 us)
Async XLA Ops:
  0.6 6.3 %copy-start = (bf16[1792,256]{1,0:T(8,128)(2,1)S(1)}, bf16[1792,256]{1,0:T(8,128)(2,1)}, u32[]{:S(2)}) copy-start(bf16[1792,256]{1,0:T(8,128)(2,1)} %param.5) | copy-start | bytes 2752516
  2.0 11.5 %all-to-all-start.2 = ((f32[4,1,64]{2,1,0:T(1,128)}), f32[4,1,64]{2,1,0:T(1,128)S(1)}, u32[]{:S(2)}, u32[]{:S(2)}) async-start(f32[4,1,64]{2,1,0:T(1,128)} %broadcast_in_dim.19), calls=%async_computation.2 | async-start | bytes 4096 | tf_op jit(solution)/shard_map/all_to_all | solution.py:24
  13.5 4.4 %copy-start.2 = (s32[2048,8]{0,1:T(8,128)S(1)}, s32[2048,8]{0,1:T(8,128)}, u32[]{:S(2)}) copy-start(s32[2048,8]{0,1:T(8,128)} %param.6) | copy-start | bytes 196612
  13.5 48.1 %all-to-all-start = ((f32[4,2048,64]{1,2,0:T(8,128)}), f32[4,2048,64]{1,2,0:T(8,128)S(1)}, u32[]{:S(2)}, u32[]{:S(2)}) async-start(f32[4,2048,64]{1,2,0:T(8,128)} %bitcast.5), calls=%async_computation | async-start | bytes 4194304 | tf_op jit(solution)/shard_map/all_to_all | solution.py:18
  60.3 14.9 %copy-start.3 = (f32[256]{0:T(256)}, f32[256]{0:T(256)S(1)}, u32[]{:S(2)}) copy-start(f32[256]{0:T(256)S(1)} %psum.23) | copy-start | bytes 3076
  61.9 13.3 %copy-start.1 = (f32[2048,64]{0,1:T(8,128)}, f32[2048,64]{0,1:T(8,128)S(1)}, u32[]{:S(2)}) copy-start(f32[2048,64]{0,1:T(8,128)S(1)} %add_divide_fusion) | copy-start | bytes 1572868
  64.1 10.4 %all-to-all-start.1 = ((f32[4,2048,8]{1,2,0:T(8,128)}), f32[4,2048,8]{1,2,0:T(8,128)S(1)}, u32[]{:S(2)}, u32[]{:S(2)}) async-start(f32[4,2048,8]{1,2,0:T(8,128)} %broadcast_in_dim.18), calls=%async_computation.1 | async-start | bytes 524288 | tf_op jit(solution)/shard_map/all_to_all | solution.py:24
where the time goes:
time: 75.9 us; the launch traced here: 75.2 us
  blocking collectives  34.1 us (45%)
  starting transfers between devices  13.9 us (18%)
  other arithmetic  10.7 us (14%)
  matrix products  6.54 us (9%)
  waiting for transfers between devices  5.28 us (7%)
  local copies, waits for them, and re-layouts  3.97 us (5%)
    psum x3, blocking collectives, over_axes(): shard = lax.psum(shard, axis)  34.1 us
    all_to_all x2, starting transfers between devices, copy_for_each(): lax.all_to_all(jnp.broadcast_to(shard[None], (length, *shard.shape)), axi...  9.52 us
    reduce_sum x1, other arithmetic, count_experts(): return jnp.sum(matches.astype(jnp.float32), axis=(0, 1))  7.01 us
    dot_general x1, matrix products, local(): jnp.dot(tokens, gate_weight, preferred_element_type=jnp.float32)  6.54 us
    all_to_all x2, waiting for transfers between devices, copy_for_each(): lax.all_to_all(jnp.broadcast_to(shard[None], (length, *shard.shape)), axi...  5.28 us
    all_to_all x1, starting transfers between devices, summed_on_arrival(): lax.all_to_all(pieces, axis, split_axis=0, concat_axis=0, tiled=True)  4.37 us
    broadcast_in_dim x2, local copies, waits for them, and re-layouts, copy_for_each(): jnp.broadcast_to(shard[None], (length, *shard.shape))  2.02 us
  transfers between devices with their start and end apart: 3, of which 1 were waited for; matrix products, arithmetic and copies ran while one was open for 22% of the time, Pallas kernels for 0%

commit v1 on v0

v1 whole, which is shorter than its diff:
```python
import functools

import jax
import jax.numpy as jnp
from jax import lax
from jax.experimental import pallas as pl
from jax.experimental.pallas import tpu as pltpu
from jax.sharding import Mesh
from jax.sharding import PartitionSpec as P

TOK = ("tok_0", "tok_1", "tok_2")
MESH = pl.DeviceIdType.MESH
F32 = jnp.float32
BF16 = jnp.bfloat16
I32 = jnp.int32
I16 = jnp.int16

STEPS = 3800.0
KNEE = 0.25


def encode(x):
    grade = jnp.log(jnp.abs(x) * (1.0 / KNEE) + 1.0) * STEPS + 0.5
    return jnp.where(x < 0.0, -grade, grade).astype(I32)


def decode(code):
    grade = code.astype(I32).astype(F32)
    size = jnp.exp(jnp.abs(grade) * (1.0 / STEPS)) * KNEE - KNEE
    return jnp.where(grade < 0.0, -size, size)


def sigmoid(x):
    return 1.0 / (1.0 + jnp.exp(-x))


def kernel(
    sizes, x_hbm, w_hbm, ids_hbm, bias_hbm, aff_ref, wts_ref, load_ref, new_ref,
    x_v, w_v, wt_v, ids_v, bias_v, p_v, acc_v,
    sa1, sb1, sa2, sb2, sc1, sc2, ra1, rb1, ra2, rb2, rc1, rc2,
    hot_hi, hot_lo, d0, d1, dr1, dr2, b0, b1, br1, br2,
    x_sem, in_sem, ss, rs, d1_ss, d1_rs, d2_ss, d2_rs, b_ss, b_rs, near,
):
    nz, nx, nc, chunks, width, target = sizes
    own = 64
    half = own // 2
    z, xx, core, m = (lax.axis_index(a) for a in (*TOK, "exp"))
    mate = m + 1 - 2 * (m % 2)
    cross = 3 - m
    group = nx * nc
    place = xx * nc + core

    def sibling(r):
        peer = (place + r) % group
        return {"tok_1": peer // nc, "tok_2": peer % nc}

    def along(r):
        return {"tok_0": (z + r) % nz}

    def x_copy(c):
        return pltpu.make_async_copy(
            x_hbm.at[pl.ds(pl.multiple_of(c * width, width), width), :], x_v.at[c], x_sem.at[c]
        )

    ids_copy = pltpu.make_async_copy(ids_hbm, ids_v, in_sem.at[0])
    w_copy = pltpu.make_async_copy(w_hbm, w_v, in_sem.at[1])
    bias_copy = pltpu.make_async_copy(bias_hbm, bias_v, in_sem.at[2])
    ids_copy.start()
    w_copy.start()
    bias_copy.start()
    for c in range(chunks):
        x_copy(c).start()

    barrier = pltpu.get_barrier_semaphore()
    steps = sorted({s % nz for s in (1, 2, -1, -2)} - {0})
    partners = [{"exp": mate}, {"exp": cross}]
    partners += [sibling(r) for r in range(1, group)]
    partners += [along(s) for s in steps]
    for partner in partners:
        pl.semaphore_signal(barrier, inc=1, device_id=partner, device_id_type=MESH)

    ids_copy.wait()
    digits = lax.broadcasted_iota(I32, (16, 8, width), 0)

    def count(c, total):
        ids = ids_v[:, pl.ds(pl.multiple_of(c * width, width), width)]
        hi, lo = ids >> 4, ids & 15
        one_hi = jnp.where(hi[None] == digits, 1.0, 0.0).reshape(128, width).astype(BF16)
        one_lo = jnp.where(lo[None] == digits, 1.0, 0.0).reshape(128, width).astype(BF16)
        return total + lax.dot_general(
            one_hi, one_lo, (((1,), (1,)), ((), ())), preferred_element_type=F32
        )

    pairs = lax.fori_loop(0, chunks, count, jnp.zeros((128, 128), F32))
    row = lax.broadcasted_iota(I32, (128, 128), 0)
    col = lax.broadcasted_iota(I32, (128, 128), 1)
    by_slot = jnp.where(row % 8 == col % 8, pairs, 0.0).reshape(16, 8, 128).sum(axis=1)
    fold = jnp.where(row // 8 == col % 16, 1.0, 0.0).astype(BF16)
    upper = jnp.floor(by_slot * (1.0 / 64.0))
    lower = by_slot - 64.0 * upper
    counts = 64.0 * jnp.dot(upper.astype(BF16), fold, preferred_element_type=F32) + jnp.dot(
        lower.astype(BF16), fold, preferred_element_type=F32
    )
    sub = lax.broadcasted_iota(I32, (8, 128), 0)
    lane = lax.broadcasted_iota(I32, (8, 128), 1)
    pick = lane // 16 == sub
    first = jnp.sum(jnp.where(pick, counts[:8], 0.0), axis=0, keepdims=True)
    second = jnp.sum(jnp.where(pick, counts[8:], 0.0), axis=0, keepdims=True)
    d0[...] = jnp.where(sub == 0, first, jnp.where(sub == 1, second, 0.0))

    bias_copy.wait()
    mine = bias_v[...]
    mine = jnp.broadcast_to(jnp.concatenate([mine, mine], axis=1), (8, 128))
    b0[...] = jnp.where((sub == m // 2) & (lane // own == m % 2), mine, 0.0)

    w_copy.wait()
    wt_v[...] = w_v[...].T

    low_a = jnp.where(m % 3 == 0, 1, 0)
    low_b = jnp.where(m < 2, 2, 0)
    pos_a = jnp.where(m < 2, 0, 1)
    pos_b = m % 2

    def part(c, block, second_half):
        return p_v[c, pl.ds(pl.multiple_of(block * own + second_half * half, half), half), :]

    def compute(c):
        x_copy(c).wait()
        p_v[c] = lax.dot_general(
            wt_v[...], x_v[c], (((1,), (1,)), ((), ())), preferred_element_type=F32
        )
        sa1[c, :half] = encode(part(c, low_a, 0)).astype(I16)
        sa1[c, half:] = encode(part(c, 3 - low_a, 0)).astype(I16)
        sb1[c, :half] = encode(part(c, low_b, 1)).astype(I16)
        sb1[c, half:] = encode(part(c, low_b + 1, 1)).astype(I16)
        ids = ids_v[:, pl.ds(pl.multiple_of(c * width, width), width)]
        tile, within = ids >> 3, ids & 7
        chosen = jnp.zeros((8, width), F32)
        for k in range(4 * own // 8):
            rows = p_v[c, 8 * k : 8 * k + 8, :]
            got = jnp.take_along_axis(rows, within, axis=0, mode="promise_in_bounds")
            chosen = jnp.where(tile == k, got, chosen)
        code = encode(chosen)
        sc1[c] = jnp.concatenate(
            [code[:, 128 * i : 128 * (i + 1)] for i in range(width // 128)], axis=0
        ).astype(I16)

    def remote(src, dst, c, kind, partner):
        return pltpu.make_async_remote_copy(
            src_ref=src.at[c],
            dst_ref=dst.at[c],
            send_sem=ss.at[kind, c],
            recv_sem=rs.at[kind, c],
            device_id={"exp": partner},
            device_id_type=MESH,
        )

    def even(c):
        return jnp.where(c % 2 == 0, mate, cross)

    def odd(c):
        return jnp.where(c % 2 == 0, cross, mate)

    def copies_1(c):
        return (
            remote(sa1, ra1, c, 0, mate),
            remote(sb1, rb1, c, 1, cross),
            remote(sc1, rc1, c, 2, even(c)),
        )

    def copies_2(c):
        return (
            remote(sa2, ra2, c, 3, cross),
            remote(sb2, rb2, c, 4, mate),
            remote(sc2, rc2, c, 5, odd(c)),
        )

    def send(copies):
        for copy in copies:
            copy.start()

    def count_copies_1(r):
        return pltpu.make_async_remote_copy(
            src_ref=d0, dst_ref=dr1.at[r - 1], send_sem=d1_ss.at[r - 1], recv_sem=d1_rs.at[r - 1],
            device_id=sibling(r), device_id_type=MESH,
        )

    def count_copies_2(r):
        return pltpu.make_async_remote_copy(
            src_ref=d1, dst_ref=dr2.at[r - 1], send_sem=d2_ss.at[r - 1], recv_sem=d2_rs.at[r - 1],
            device_id=along(r), device_id_type=MESH,
        )

    def bias_copy_to(src, dst, i, partner):
        return pltpu.make_async_remote_copy(
            src_ref=src, dst_ref=dst, send_sem=b_ss.at[i], recv_sem=b_rs.at[i],
            device_id={"exp": partner}, device_id_type=MESH,
        )

    compute(0)
    pl.semaphore_wait(barrier, len(partners))
    send(copies_1(0))
    for r in range(1, group):
        count_copies_1(r).start()
    bias_copy_to(b0, br1, 0, mate).start()
    far = sorted({s % nz for s in (2, -2)} - {0})
    for s in far:
        pl.semaphore_signal(near, inc=1, device_id=along(s), device_id_type=MESH)

    @pl.loop(1, chunks)
    def _(c):
        compute(c)
        send(copies_1(c))

    for r in range(1, group):
        count_copies_1(r).wait_recv()
    d1[...] = sum((dr1[r - 1] for r in range(1, group)), d0[...])
    bias_copy_to(b0, br1, 0, mate).wait_recv()
    b1[...] = b0[...] + br1[...]
    pl.semaphore_wait(near, len(far))
    for r in range(1, nz):
        count_copies_2(r).start()
    bias_copy_to(b1, br2, 1, cross).start()

    @pl.loop(0, chunks)
    def _(c):
        for copy in copies_1(c):
            copy.wait_recv()
        at_a = pl.multiple_of(pos_a * half, half)
        at_b = pl.multiple_of(pos_b * half, half)
        off_a = pl.multiple_of((1 - pos_a) * half, half)
        off_b = pl.multiple_of((1 - pos_b) * half, half)
        sa2[c] = encode(part(c, cross, 0) + decode(ra1[c, pl.ds(off_a, half), :])).astype(I16)
        sb2[c] = encode(part(c, mate, 1) + decode(rb1[c, pl.ds(off_b, half), :])).astype(I16)
        sc2[c] = encode(decode(sc1[c]) + decode(rc1[c])).astype(I16)
        acc_v[c, :half] = part(c, m, 0) + decode(ra1[c, pl.ds(at_a, half), :])
        acc_v[c, half:] = part(c, m, 1) + decode(rb1[c, pl.ds(at_b, half), :])
        send(copies_2(c))

    for r in range(1, nz):
        count_copies_2(r).wait_recv()
    bias_copy_to(b1, br2, 1, cross).wait_recv()
    load = sum((dr2[r - 1] for r in range(1, nz)), d1[...])
    gap = target - (4.0 * own) * load
    sign = jnp.where(gap > 0.0, 1.0, jnp.where(gap < 0.0, -1.0, 0.0))
    new_bias = (b1[...] + br2[...]) + 0.001 * sign
    for i in range(2):
        load_ref[:, 128 * i : 128 * (i + 1)] = load[i : i + 1]
        new_ref[:, 128 * i : 128 * (i + 1)] = new_bias[i : i + 1]

    @pl.loop(0, chunks)
    def _(c):
        for copy in copies_2(c):
            copy.wait_recv()
        at = pl.multiple_of(c * width, width)
        aff_ref[:half, pl.ds(at, width)] = sigmoid(acc_v[c, :half] + decode(ra2[c]))
        aff_ref[half:, pl.ds(at, width)] = sigmoid(acc_v[c, half:] + decode(rb2[c]))
        chosen = sigmoid(decode(sc2[c]) + decode(rc2[c]))
        for i in range(width // 128):
            values = chosen[8 * i : 8 * i + 8]
            total = jnp.sum(values, axis=0, keepdims=True)
            wts_ref[:, pl.ds(pl.multiple_of(at + 128 * i, 128), 128)] = 2.5 * values / total

    @pl.loop(0, chunks)
    def _(c):
        for copy in (*copies_1(c), *copies_2(c)):
            copy.wait_send()

    for r in range(1, group):
        count_copies_1(r).wait_send()
    for r in range(1, nz):
        count_copies_2(r).wait_send()
    bias_copy_to(b0, br1, 0, mate).wait_send()
    bias_copy_to(b1, br2, 1, cross).wait_send()


def hand_out(*refs):
    count = len(refs) // 2
    copies = [
        pltpu.make_async_copy(refs[i], refs[count + i], refs[-1].at[i]) for i in range(count)
    ]
    for copy in copies:
        copy.start()
    for copy in copies:
        copy.wait()


def local(shape, tokens, gate_weight, expert_ids, expert_bias):
    nz, nx, nc = shape
    rows, depth = tokens.shape
    experts = gate_weight.shape[1]
    slots = expert_ids.shape[1]
    width = 256
    chunks = rows // width
    own = experts // 4
    target = float(rows * nz * nx * nc * slots)
    sizes = (nz, nx, nc, chunks, width, target)
    dma = pltpu.SemaphoreType.DMA
    big = pltpu.VMEM((chunks, own, width), I16)
    small = pltpu.VMEM((chunks, own // 2, width), I16)
    few = pltpu.VMEM((chunks, 16, 128), I16)
    tile = pltpu.VMEM((8, 128), F32)
    group = nx * nc
    made = pl.pallas_call(
        functools.partial(kernel, sizes),
        out_shape=(
            pltpu.VMEM((own, rows), F32),
            pltpu.VMEM((slots, rows), F32),
            pltpu.VMEM((1, experts), F32),
            pltpu.VMEM((1, experts), F32),
        ),
        in_specs=[pl.BlockSpec(memory_space=pltpu.HBM)] * 4,
        out_specs=(pl.BlockSpec(memory_space=pltpu.VMEM),) * 4,
        scratch_shapes=[
            pltpu.VMEM((chunks, width, depth), BF16),
            pltpu.VMEM((depth, experts), BF16),
            pltpu.VMEM((experts, depth), BF16),
            pltpu.VMEM((slots, rows), I32),
            pltpu.VMEM((1, own), F32),
            pltpu.VMEM((chunks, experts, width), F32),
            pltpu.VMEM((chunks, own, width), F32),
            big, big, small, small, few, few, big, big, small, small, few, few,
            pltpu.VMEM((128, width), BF16), pltpu.VMEM((128, width), BF16),
            tile, tile,
            pltpu.VMEM((max(group - 1, 1), 8, 128), F32), pltpu.VMEM((max(nz - 1, 1), 8, 128), F32),
            tile, tile, tile, tile,
            dma((chunks,)), dma((3,)), dma((6, chunks)), dma((6, chunks)),
            dma((max(group - 1, 1),)), dma((max(group - 1, 1),)),
            dma((max(nz - 1, 1),)), dma((max(nz - 1, 1),)),
            dma((2,)), dma((2,)), pltpu.SemaphoreType.REGULAR,
        ],
        compiler_params=pltpu.CompilerParams(
            collective_id=0, has_side_effects=True, vmem_limit_bytes=66300000
        ),
        name="router",
    )(tokens, gate_weight, expert_ids.T, expert_bias.reshape(1, own))
    aff, wts, load, new = pl.pallas_call(
        hand_out,
        out_shape=tuple(jax.ShapeDtypeStruct(a.shape, a.dtype) for a in made),
        in_specs=[pl.BlockSpec(memory_space=pltpu.VMEM)] * 4,
        out_specs=(pl.BlockSpec(memory_space=pltpu.HBM),) * 4,
        scratch_shapes=[dma((4,))],
        compiler_params=pltpu.CompilerParams(vmem_limit_bytes=2**20),
        name="hand_out",
    )(*made)
    return aff.T, wts.T, load.reshape(experts), new.reshape(experts)


def solution(mesh):
    shape = (8, 4, 2)
    split = Mesh(mesh.devices.reshape(*shape, mesh.shape["exp"]), (*TOK, "exp"))
    in_specs = (P(TOK, "exp"), P("exp", None), P(TOK, None), P("exp"))
    out_specs = (P(TOK, "exp"), P(TOK, None), P(), P())
    return jax.shard_map(
        functools.partial(local, shape),
        mesh=split, in_specs=in_specs, out_specs=out_specs, check_vma=False,
    )
```

time: 75.9 us -> 22.8 us (0.30)
  blocking collectives: 34.1 us -> 0 us
  Pallas kernels: 0 us -> 22.1 us
  starting transfers between devices: 13.9 us -> 0 us
  other arithmetic: 10.7 us -> 0 us
  matrix products: 6.54 us -> 0 us
  waiting for transfers between devices: 5.28 us -> 0 us
  local copies, waits for them, and re-layouts: 3.97 us -> 0 us
    psum x3 -> x0, blocking collectives: 34.1 us -> none  [over_axes(): shard = lax.psum(shard, axis)]
    pallas_call x0 -> x2, Pallas kernels: none -> 22.1 us  [the longest x1 21.3 us: local(): pl.pallas_call(functools.partial(kernel, sizes), out_shape=(pltpu.VMEM((o...]
    all_to_all x3 -> x0, starting transfers between devices: 13.9 us -> none  [the longest x2 9.52 us: copy_for_each(): lax.all_to_all(jnp.broadcast_to(shard[None], (length, *shard.shape)), axi...]
    reduce_sum x4 -> x0, other arithmetic: 8.69 us -> none  [the longest x1 7.01 us: count_experts(): return jnp.sum(matches.astype(jnp.float32), axis=(0, 1))]
    dot_general x1 -> x0, matrix products: 6.54 us -> none  [local(): jnp.dot(tokens, gate_weight, preferred_element_type=jnp.float32)]
    all_to_all x3 -> x0, waiting for transfers between devices: 5.28 us -> none  [the longest x2 5.28 us: copy_for_each(): lax.all_to_all(jnp.broadcast_to(shard[None], (length, *shard.shape)), axi...]
    broadcast_in_dim x2 -> x0, local copies, waits for them, and re-layouts: 2.02 us -> none  [copy_for_each(): jnp.broadcast_to(shard[None], (length, *shard.shape))]
    unnamed x9 -> x0, local copies, waits for them, and re-layouts: 1.35 us -> none
  transfers between devices with their start and end apart: 3 -> 0, of which waited for: 1 -> 0; matrix products, arithmetic and copies ran while one was open for 22% -> 0% of each run, Pallas kernels for 0% -> 0%
where the time goes in v1:
time: 22.8 us; the launch traced here: 22.7 us
  Pallas kernels  22.1 us (97%)
  between operations  0.64 us (3%)
    pallas_call x1, Pallas kernels, local(): pl.pallas_call(functools.partial(kernel, sizes), out_shape=(pltpu.VMEM((o...  21.3 us
    pallas_call x1, Pallas kernels, local(): pl.pallas_call(hand_out, out_shape=tuple((jax.ShapeDtypeStruct(a.shape, a...  0.84 us

profile of v1, /device:TPU:1, one launch (start us, length us, event | category | flops | bytes accessed | tf_op | source)
XLA Modules:
  0.0 22.7 jit_solution(13051224923790088264)
XLA Ops:
  0.6 21.3 %router.1 = (f32[64,2048]{1,0:T(8,128)S(1)}, f32[8,2048]{1,0:T(8,128)S(1)}, f32[1,256]{1,0:T(1,128)S(1)}, f32[1,256]{1,0:T(1,128)S(1)}) custom-call(bf16[2048,1792]{1,0:T(8,128)(2,1)} %x_hbm.1, bf16[1792,256]{1,0:T(8,128)(2,1)} %w_hbm.1, s32[8,2048]{1,0:T(8,128)} %bitcast.6, f32[1,64]{1,0:T(1,128)} %bitcast.7), custom_call_target="tpu_custom_call" | custom-call | tf_op jit(solution)/shard_map/router/pallas_call | solution.py:304
  21.9 0.8 %hand_out.1 = (f32[64,2048]{1,0:T(8,128)}, f32[8,2048]{1,0:T(8,128)}, f32[1,256]{1,0:T(1,128)}, f32[1,256]{1,0:T(1,128)}) custom-call(f32[64,2048]{1,0:T(8,128)S(1)} %get-tuple-element.12.refs_0_, f32[8,2048]{1,0:T(8,128)S(1)} %get-tuple-element.13.refs_1_, f32[1,256]{1,0:T(1,128)S(1)} %get-tuple-element.14.refs_2_, f32[1,256]{1,0:T(1,128)S(1)} %get-tuple-element.15.refs_3_), custom_call_target="tpu_custom_call" | custom-call | tf_op jit(solution)/shard_map/hand_out/pallas_call | solution.py:337

commit v2 on v1

--- a/solution.py
+++ b/solution.py
@@ -38,24 +38,26 @@
     sizes, x_hbm, w_hbm, ids_hbm, bias_hbm, aff_ref, wts_ref, load_ref, new_ref,
     x_v, w_v, wt_v, ids_v, bias_v, p_v, acc_v,
     sa1, sb1, sa2, sb2, sc1, sc2, ra1, rb1, ra2, rb2, rc1, rc2,
-    hot_hi, hot_lo, d0, d1, dr1, dr2, b0, b1, br1, br2,
-    x_sem, in_sem, ss, rs, d1_ss, d1_rs, d2_ss, d2_rs, b_ss, b_rs, near,
+    hot_hi, hot_lo, d0, d1, u1, u2, total, near_by, above, below, b0, b1, br1, br2,
+    x_sem, in_sem, ss, rs, near_ss, near_rs, down_ss, down_rs, up_ss, up_rs, b_ss, b_rs, o_sem, wave, crest_1, crest_2,
 ):
     nz, nx, nc, chunks, width, target = sizes
     own = 64
     half = own // 2
     z, xx, core, m = (lax.axis_index(a) for a in (*TOK, "exp"))
-    mate = m + 1 - 2 * (m % 2)
+    even_y = lax.rem(m, 2) == 0
+    mate = jnp.where(even_y, m + 1, m - 1)
     cross = 3 - m
-    group = nx * nc
-    place = xx * nc + core
+    lead = core == 1
+    siblings = [(dx, dc) for dx in range(nx) for dc in range(nc)][1:]
+
+    def turned(at, by, length):
+        there = at + by
+        return jnp.where(there >= length, there - length, there)
 
     def sibling(r):
-        peer = (place + r) % group
-        return {"tok_1": peer // nc, "tok_2": peer % nc}
-
-    def along(r):
-        return {"tok_0": (z + r) % nz}
+        dx, dc = siblings[r]
+        return {"tok_1": turned(xx, dx, nx), "tok_2": turned(core, dc, nc)}
 
     def x_copy(c):
         return pltpu.make_async_copy(
@@ -67,35 +69,48 @@
     bias_copy = pltpu.make_async_copy(bias_hbm, bias_v, in_sem.at[2])
     ids_copy.start()
     w_copy.start()
+    x_copy(0).start()
     bias_copy.start()
-    for c in range(chunks):
-        x_copy(c).start()
 
     barrier = pltpu.get_barrier_semaphore()
-    steps = sorted({s % nz for s in (1, 2, -1, -2)} - {0})
-    partners = [{"exp": mate}, {"exp": cross}]
-    partners += [sibling(r) for r in range(1, group)]
-    partners += [along(s) for s in steps]
-    for partner in partners:
+
+    def greet(partner):
         pl.semaphore_signal(barrier, inc=1, device_id=partner, device_id_type=MESH)
+
+    greet({"exp": mate})
+    greet({"exp": cross})
+    for r in range(len(siblings)):
+        if siblings[r] == (0, 1):
+            greet(sibling(r))
+        else:
+            pl.when(lead)(functools.partial(lambda r: greet(sibling(r)), r))
+    pl.when(lead & (z > 0))(lambda: greet({"tok_0": z - 1}))
+    pl.when(lead & (z < nz - 1))(lambda: greet({"tok_0": z + 1}))
+    greeted = (
+        2
+        + nx
+        + jnp.where(lead & (z > 0), 1, 0)
+        + jnp.where(lead & (z < nz - 1), 1, 0)
+    ).astype(I32)
 
     ids_copy.wait()
     digits = lax.broadcasted_iota(I32, (16, 8, width), 0)
 
-    def count(c, total):
-        ids = ids_v[:, pl.ds(pl.multiple_of(c * width, width), width)]
+    @pl.loop(0, chunks)
+    def _(c):
+        at = pl.ds(pl.multiple_of(c * width, width), width)
+        ids = ids_v[:, at]
         hi, lo = ids >> 4, ids & 15
-        one_hi = jnp.where(hi[None] == digits, 1.0, 0.0).reshape(128, width).astype(BF16)
-        one_lo = jnp.where(lo[None] == digits, 1.0, 0.0).reshape(128, width).astype(BF16)
-        return total + lax.dot_general(
-            one_hi, one_lo, (((1,), (1,)), ((), ())), preferred_element_type=F32
-        )
-
-    pairs = lax.fori_loop(0, chunks, count, jnp.zeros((128, 128), F32))
+        hot_hi[:, at] = jnp.where(hi[None] == digits, 1.0, 0.0).reshape(128, width).astype(BF16)
+        hot_lo[:, at] = jnp.where(lo[None] == digits, 1.0, 0.0).reshape(128, width).astype(BF16)
+
+    pairs = lax.dot_general(
+        hot_hi[...], hot_lo[...], (((1,), (1,)), ((), ())), preferred_element_type=F32
+    )
     row = lax.broadcasted_iota(I32, (128, 128), 0)
     col = lax.broadcasted_iota(I32, (128, 128), 1)
-    by_slot = jnp.where(row % 8 == col % 8, pairs, 0.0).reshape(16, 8, 128).sum(axis=1)
-    fold = jnp.where(row // 8 == col % 16, 1.0, 0.0).astype(BF16)
+    by_slot = jnp.where((row & 7) == (col & 7), pairs, 0.0).reshape(16, 8, 128).sum(axis=1)
+    fold = jnp.where((row >> 3) == (col & 15), 1.0, 0.0).astype(BF16)
     upper = jnp.floor(by_slot * (1.0 / 64.0))
     lower = by_slot - 64.0 * upper
     counts = 64.0 * jnp.dot(upper.astype(BF16), fold, preferred_element_type=F32) + jnp.dot(
@@ -103,29 +118,24 @@
     )
     sub = lax.broadcasted_iota(I32, (8, 128), 0)
     lane = lax.broadcasted_iota(I32, (8, 128), 1)
-    pick = lane // 16 == sub
+    pick = (lane >> 4) == sub
     first = jnp.sum(jnp.where(pick, counts[:8], 0.0), axis=0, keepdims=True)
     second = jnp.sum(jnp.where(pick, counts[8:], 0.0), axis=0, keepdims=True)
     d0[...] = jnp.where(sub == 0, first, jnp.where(sub == 1, second, 0.0))
 
-    bias_copy.wait()
-    mine = bias_v[...]
-    mine = jnp.broadcast_to(jnp.concatenate([mine, mine], axis=1), (8, 128))
-    b0[...] = jnp.where((sub == m // 2) & (lane // own == m % 2), mine, 0.0)
-
     w_copy.wait()
+    x_copy(1).start()
     wt_v[...] = w_v[...].T
 
-    low_a = jnp.where(m % 3 == 0, 1, 0)
+    low_a = jnp.where((m == 0) | (m == 3), 1, 0)
     low_b = jnp.where(m < 2, 2, 0)
     pos_a = jnp.where(m < 2, 0, 1)
-    pos_b = m % 2
+    pos_b = jnp.where(even_y, 0, 1)
 
     def part(c, block, second_half):
         return p_v[c, pl.ds(pl.multiple_of(block * own + second_half * half, half), half), :]
 
     def compute(c):
-        x_copy(c).wait()
         p_v[c] = lax.dot_general(
             wt_v[...], x_v[c], (((1,), (1,)), ((), ())), preferred_element_type=F32
         )
@@ -133,6 +143,8 @@
         sa1[c, half:] = encode(part(c, 3 - low_a, 0)).astype(I16)
         sb1[c, :half] = encode(part(c, low_b, 1)).astype(I16)
         sb1[c, half:] = encode(part(c, low_b + 1, 1)).astype(I16)
+
+    def choose(c):
         ids = ids_v[:, pl.ds(pl.multiple_of(c * width, width), width)]
         tile, within = ids >> 3, ids & 7
         chosen = jnp.zeros((8, width), F32)
@@ -156,17 +168,19 @@
         )
 
     def even(c):
-        return jnp.where(c % 2 == 0, mate, cross)
+        return jnp.where(lax.rem(c, 2) == 0, mate, cross)
 
     def odd(c):
-        return jnp.where(c % 2 == 0, cross, mate)
+        return jnp.where(lax.rem(c, 2) == 0, cross, mate)
+
+    def copies_ab(c):
+        return remote(sa1, ra1, c, 0, mate), remote(sb1, rb1, c, 1, cross)
+
+    def copy_c(c):
+        return remote(sc1, rc1, c, 2, even(c))
 
     def copies_1(c):
-        return (
-            remote(sa1, ra1, c, 0, mate),
-            remote(sb1, rb1, c, 1, cross),
-            remote(sc1, rc1, c, 2, even(c)),
-        )
+        return (*copies_ab(c), copy_c(c))
 
     def copies_2(c):
         return (
@@ -179,16 +193,47 @@
         for copy in copies:
             copy.start()
 
-    def count_copies_1(r):
+    def stage_1(c):
+        compute(c)
+        send(copies_ab(c))
+        choose(c)
+        copy_c(c).start()
+
+    def count_copy(src, dst, r, sems, partner):
         return pltpu.make_async_remote_copy(
-            src_ref=d0, dst_ref=dr1.at[r - 1], send_sem=d1_ss.at[r - 1], recv_sem=d1_rs.at[r - 1],
-            device_id=sibling(r), device_id_type=MESH,
-        )
-
-    def count_copies_2(r):
+            src_ref=src, dst_ref=dst.at[r], send_sem=sems[0].at[r], recv_sem=sems[1].at[r],
+            device_id=partner, device_id_type=MESH,
+        )
+
+    def near_copy(r):
+        return count_copy(d0, near_by, r, (near_ss, near_rs), sibling(r))
+
+    def down_copy(r):
+        return count_copy(d1, above, r, (down_ss, down_rs), {"tok_0": z - r - 1})
+
+    def up_copy(i):
+        src = (d1, u1, u2)[i]
+        return count_copy(src, below, i, (up_ss, up_rs), {"tok_0": z + (1, 2, 4)[i]})
+
+    def tell(sem, there):
+        pl.semaphore_signal(sem, inc=1, device_id={"tok_0": there}, device_id_type=MESH)
+
+    def when_lower(action):
+        for r in range(nz - 1):
+            pl.when(lead & (z > r))(functools.partial(action, r))
+
+    def when_upper(action):
+        for r in range(nz - 1):
+            pl.when(lead & (z + r + 1 < nz))(functools.partial(action, r))
+
+    def near_sends(action):
+        for r in range(len(siblings)):
+            pl.when(core == 1 - siblings[r][1])(functools.partial(action, r))
+
+    def hand_over():
         return pltpu.make_async_remote_copy(
-            src_ref=d1, dst_ref=dr2.at[r - 1], send_sem=d2_ss.at[r - 1], recv_sem=d2_rs.at[r - 1],
-            device_id=along(r), device_id_type=MESH,
+            src_ref=total, dst_ref=total, send_sem=o_sem.at[0], recv_sem=o_sem.at[1],
+            device_id={"tok_2": 1 - core}, device_id_type=MESH,
         )
 
     def bias_copy_to(src, dst, i, partner):
@@ -197,33 +242,47 @@
             device_id={"exp": partner}, device_id_type=MESH,
         )
 
+    x_copy(0).wait()
+    x_copy(2).start()
     compute(0)
-    pl.semaphore_wait(barrier, len(partners))
-    send(copies_1(0))
-    for r in range(1, group):
-        count_copies_1(r).start()
+    pl.semaphore_wait(barrier, greeted)
+    send(copies_ab(0))
+    near_sends(lambda r: near_copy(r).start())
+    x_copy(3).start()
+    choose(0)
+    copy_c(0).start()
+
+    bias_copy.wait()
+    mine = bias_v[...]
+    mine = jnp.broadcast_to(jnp.concatenate([mine, mine], axis=1), (8, 128))
+    my_row = jnp.where(m < 2, 0, 1)
+    b0[...] = jnp.where((sub == my_row) & ((lane >> 6) == pos_b), mine, 0.0)
+
+
+    x_copy(1).wait()
+    x_copy(4).start()
+    stage_1(1)
     bias_copy_to(b0, br1, 0, mate).start()
-    far = sorted({s % nz for s in (2, -2)} - {0})
-    for s in far:
-        pl.semaphore_signal(near, inc=1, device_id=along(s), device_id_type=MESH)
-
-    @pl.loop(1, chunks)
-    def _(c):
-        compute(c)
-        send(copies_1(c))
-
-    for r in range(1, group):
-        count_copies_1(r).wait_recv()
-    d1[...] = sum((dr1[r - 1] for r in range(1, group)), d0[...])
+
+    def later(c):
+        x_copy(c).wait()
+
+        @pl.when(c + 3 < chunks)
+        def _():
+            x_copy(c + 3).start()
+
+        stage_1(c)
+
+    pl.loop(2, chunks)(later)
+
+    pl.when(lead & (z > 0))(lambda: pl.semaphore_wait(wave, 1))
+    pl.when(lead & (z < nz - 1))(lambda: tell(wave, z + 1))
+
     bias_copy_to(b0, br1, 0, mate).wait_recv()
     b1[...] = b0[...] + br1[...]
-    pl.semaphore_wait(near, len(far))
-    for r in range(1, nz):
-        count_copies_2(r).start()
     bias_copy_to(b1, br2, 1, cross).start()
 
-    @pl.loop(0, chunks)
-    def _(c):
+    def combine(c):
         for copy in copies_1(c):
             copy.wait_recv()
         at_a = pl.multiple_of(pos_a * half, half)
@@ -237,19 +296,33 @@
         acc_v[c, half:] = part(c, m, 1) + decode(rb1[c, pl.ds(at_b, half), :])
         send(copies_2(c))
 
-    for r in range(1, nz):
-        count_copies_2(r).wait_recv()
-    bias_copy_to(b1, br2, 1, cross).wait_recv()
-    load = sum((dr2[r - 1] for r in range(1, nz)), d1[...])
-    gap = target - (4.0 * own) * load
-    sign = jnp.where(gap > 0.0, 1.0, jnp.where(gap < 0.0, -1.0, 0.0))
-    new_bias = (b1[...] + br2[...]) + 0.001 * sign
-    for i in range(2):
-        load_ref[:, 128 * i : 128 * (i + 1)] = load[i : i + 1]
-        new_ref[:, 128 * i : 128 * (i + 1)] = new_bias[i : i + 1]
-
-    @pl.loop(0, chunks)
-    def _(c):
+    pl.loop(0, 3)(combine)
+
+    @pl.when(lead)
+    def _():
+        for r in range(len(siblings)):
+            near_copy(r).wait_recv()
+        d1[...] = sum((near_by[r] for r in range(len(siblings))), d0[...])
+
+    when_lower(lambda r: down_copy(r).start())
+    pl.when(lead & (z + 1 < nz))(lambda: up_copy(0).start())
+    pl.when(lead & (z >= 1))(lambda: tell(crest_1, z - 1))
+
+    pl.loop(3, 6)(combine)
+
+    pl.when(lead & (z >= 1))(lambda: up_copy(0).wait_recv())
+
+    @pl.when(lead)
+    def _():
+        u1[...] = d1[...] + jnp.where(z >= 1, below[0], 0.0)
+
+    pl.when(lead & (z + 1 < nz))(lambda: pl.semaphore_wait(crest_1, 1))
+    pl.when(lead & (z + 2 < nz))(lambda: up_copy(1).start())
+    pl.when(lead & (z >= 2))(lambda: tell(crest_2, z - 2))
+
+    pl.loop(6, chunks)(combine)
+
+    def finish(c):
         for copy in copies_2(c):
             copy.wait_recv()
         at = pl.multiple_of(c * width, width)
@@ -261,15 +334,51 @@
             total = jnp.sum(values, axis=0, keepdims=True)
             wts_ref[:, pl.ds(pl.multiple_of(at + 128 * i, 128), 128)] = 2.5 * values / total
 
+    pl.loop(0, 3)(finish)
+
+    pl.when(lead & (z >= 2))(lambda: up_copy(1).wait_recv())
+
+    @pl.when(lead)
+    def _():
+        u2[...] = u1[...] + jnp.where(z >= 2, below[1], 0.0)
+
+    pl.when(lead & (z + 2 < nz))(lambda: pl.semaphore_wait(crest_2, 1))
+    pl.when(lead & (z + 4 < nz))(lambda: up_copy(2).start())
+
+    pl.loop(3, chunks)(finish)
+
+    pl.when(lead & (z >= 4))(lambda: up_copy(2).wait_recv())
+    when_upper(lambda r: down_copy(r).wait_recv())
+
+    @pl.when(lead)
+    def _():
+        load = u2[...] + jnp.where(z >= 4, below[2], 0.0)
+        for r in range(nz - 1):
+            load = load + jnp.where(z + r + 1 < nz, above[r], 0.0)
+        total[...] = load
+        hand_over().start()
+
+    pl.when(core == 0)(lambda: hand_over().wait_recv())
+    bias_copy_to(b1, br2, 1, cross).wait_recv()
+    load = total[...]
+    gap = target - (4.0 * own) * load
+    sign = jnp.where(gap > 0.0, 1.0, jnp.where(gap < 0.0, -1.0, 0.0))
+    new_bias = (b1[...] + br2[...]) + 0.001 * sign
+    for i in range(2):
+        load_ref[:, 128 * i : 128 * (i + 1)] = load[i : i + 1]
+        new_ref[:, 128 * i : 128 * (i + 1)] = new_bias[i : i + 1]
+
     @pl.loop(0, chunks)
     def _(c):
         for copy in (*copies_1(c), *copies_2(c)):
             copy.wait_send()
 
-    for r in range(1, group):
-        count_copies_1(r).wait_send()
-    for r in range(1, nz):
-        count_copies_2(r).wait_send()
+    near_sends(lambda r: near_copy(r).wait_send())
+    pl.when(lead)(lambda: hand_over().wait_send())
+    when_lower(lambda r: down_copy(r).wait_send())
+    pl.when(lead & (z + 1 < nz))(lambda: up_copy(0).wait_send())
+    pl.when(lead & (z + 2 < nz))(lambda: up_copy(1).wait_send())
+    pl.when(lead & (z + 4 < nz))(lambda: up_copy(2).wait_send())
     bias_copy_to(b0, br1, 0, mate).wait_send()
     bias_copy_to(b1, br2, 1, cross).wait_send()
 
@@ -300,7 +409,11 @@
     small = pltpu.VMEM((chunks, own // 2, width), I16)
     few = pltpu.VMEM((chunks, 16, 128), I16)
     tile = pltpu.VMEM((8, 128), F32)
-    group = nx * nc
+
+    def tiles(n):
+        return pltpu.VMEM((n, 8, 128), F32)
+
+    group, line = nx * nc - 1, nz - 1
     made = pl.pallas_call(
         functools.partial(kernel, sizes),
         out_shape=(
@@ -320,14 +433,11 @@
             pltpu.VMEM((chunks, experts, width), F32),
             pltpu.VMEM((chunks, own, width), F32),
             big, big, small, small, few, few, big, big, small, small, few, few,
-            pltpu.VMEM((128, width), BF16), pltpu.VMEM((128, width), BF16),
-            tile, tile,
-            pltpu.VMEM((max(group - 1, 1), 8, 128), F32), pltpu.VMEM((max(nz - 1, 1), 8, 128), F32),
-            tile, tile, tile, tile,
+            pltpu.VMEM((128, rows), BF16), pltpu.VMEM((128, rows), BF16),
+            tile, tile, tile, tile, tile, tiles(group), tiles(line), tiles(3), tile, tile, tile, tile,
             dma((chunks,)), dma((3,)), dma((6, chunks)), dma((6, chunks)),
-            dma((max(group - 1, 1),)), dma((max(group - 1, 1),)),
-            dma((max(nz - 1, 1),)), dma((max(nz - 1, 1),)),
-            dma((2,)), dma((2,)), pltpu.SemaphoreType.REGULAR,
+            dma((group,)), dma((group,)), dma((line,)), dma((line,)), dma((3,)), dma((3,)),
+            dma((2,)), dma((2,)), dma((2,)), *[pltpu.SemaphoreType.REGULAR] * 3,
         ],
         compiler_params=pltpu.CompilerParams(
             collective_id=0, has_side_effects=True, vmem_limit_bytes=66300000

time: 22.8 us -> 21.7 us (0.952)
  Pallas kernels: 22.1 us -> 20.9 us
    pallas_call x1, Pallas kernels: 21.3 us -> 20.1 us  [local(): pl.pallas_call(functools.partial(kernel, sizes), out_shape=(pltpu.VMEM((o...]
where the time goes in v2:
time: 21.7 us; the launch traced here: 21.6 us
  Pallas kernels  20.9 us (96%)
  between operations  0.64 us (3%)
    pallas_call x1, Pallas kernels, local(): pl.pallas_call(functools.partial(kernel, sizes), out_shape=(pltpu.VMEM((o...  20.1 us
    pallas_call x1, Pallas kernels, local(): pl.pallas_call(hand_out, out_shape=tuple((jax.ShapeDtypeStruct(a.shape, a...  0.84 us

profile of v2, /device:TPU:1, one launch (start us, length us, event | category | flops | bytes accessed | tf_op | source)
XLA Modules:
  0.0 21.6 jit_solution(7316349063114350635)
XLA Ops:
  0.6 20.1 %router.1 = (f32[64,2048]{1,0:T(8,128)S(1)}, f32[8,2048]{1,0:T(8,128)S(1)}, f32[1,256]{1,0:T(1,128)S(1)}, f32[1,256]{1,0:T(1,128)S(1)}) custom-call(bf16[2048,1792]{1,0:T(8,128)(2,1)} %x_hbm.1, bf16[1792,256]{1,0:T(8,128)(2,1)} %w_hbm.1, s32[8,2048]{1,0:T(8,128)} %bitcast.6, f32[1,64]{1,0:T(1,128)} %bitcast.7), custom_call_target="tpu_custom_call" | custom-call | tf_op jit(solution)/shard_map/router/pallas_call | solution.py:417
  20.7 0.8 %hand_out.1 = (f32[64,2048]{1,0:T(8,128)}, f32[8,2048]{1,0:T(8,128)}, f32[1,256]{1,0:T(1,128)}, f32[1,256]{1,0:T(1,128)}) custom-call(f32[64,2048]{1,0:T(8,128)S(1)} %get-tuple-element.12.refs_0_, f32[8,2048]{1,0:T(8,128)S(1)} %get-tuple-element.13.refs_1_, f32[1,256]{1,0:T(1,128)S(1)} %get-tuple-element.14.refs_2_, f32[1,256]{1,0:T(1,128)S(1)} %get-tuple-element.15.refs_3_), custom_call_target="tpu_custom_call" | custom-call | tf_op jit(solution)/shard_map/hand_out/pallas_call | solution.py:447

commit v3 on v2

--- a/solution.py
+++ b/solution.py
@@ -39,7 +39,7 @@
     x_v, w_v, wt_v, ids_v, bias_v, p_v, acc_v,
     sa1, sb1, sa2, sb2, sc1, sc2, ra1, rb1, ra2, rb2, rc1, rc2,
     hot_hi, hot_lo, d0, d1, u1, u2, total, near_by, above, below, b0, b1, br1, br2,
-    x_sem, in_sem, ss, rs, near_ss, near_rs, down_ss, down_rs, up_ss, up_rs, b_ss, b_rs, o_sem, wave, crest_1, crest_2,
+    x_sem, in_sem, ss, rs, near_ss, near_rs, down_ss, down_rs, up_ss, up_rs, b_ss, b_rs, o_sem, crest_1, crest_2,
 ):
     nz, nx, nc, chunks, width, target = sizes
     own = 64
@@ -85,11 +85,14 @@
         else:
             pl.when(lead)(functools.partial(lambda r: greet(sibling(r)), r))
     pl.when(lead & (z > 0))(lambda: greet({"tok_0": z - 1}))
-    pl.when(lead & (z < nz - 1))(lambda: greet({"tok_0": z + 1}))
+    for r in range(nz - 1):
+        pl.when(lead & (z + r + 1 < nz))(
+            functools.partial(lambda r: greet({"tok_0": z + r + 1}), r)
+        )
     greeted = (
         2
         + nx
-        + jnp.where(lead & (z > 0), 1, 0)
+        + jnp.where(lead, z, 0)
         + jnp.where(lead & (z < nz - 1), 1, 0)
     ).astype(I32)
 
@@ -273,10 +276,19 @@
 
         stage_1(c)
 
-    pl.loop(2, chunks)(later)
-
-    pl.when(lead & (z > 0))(lambda: pl.semaphore_wait(wave, 1))
-    pl.when(lead & (z < nz - 1))(lambda: tell(wave, z + 1))
+    pl.loop(2, chunks - 1)(later)
+
+    @pl.when(lead)
+    def _():
+        for r in range(len(siblings)):
+            near_copy(r).wait_recv()
+        d1[...] = sum((near_by[r] for r in range(len(siblings))), d0[...])
+
+    when_lower(lambda r: down_copy(r).start())
+    pl.when(lead & (z + 1 < nz))(lambda: up_copy(0).start())
+    pl.when(lead & (z >= 1))(lambda: tell(crest_1, z - 1))
+
+    pl.loop(chunks - 1, chunks)(later)
 
     bias_copy_to(b0, br1, 0, mate).wait_recv()
     b1[...] = b0[...] + br1[...]
@@ -296,19 +308,7 @@
         acc_v[c, half:] = part(c, m, 1) + decode(rb1[c, pl.ds(at_b, half), :])
         send(copies_2(c))
 
-    pl.loop(0, 3)(combine)
-
-    @pl.when(lead)
-    def _():
-        for r in range(len(siblings)):
-            near_copy(r).wait_recv()
-        d1[...] = sum((near_by[r] for r in range(len(siblings))), d0[...])
-
-    when_lower(lambda r: down_copy(r).start())
-    pl.when(lead & (z + 1 < nz))(lambda: up_copy(0).start())
-    pl.when(lead & (z >= 1))(lambda: tell(crest_1, z - 1))
-
-    pl.loop(3, 6)(combine)
+    pl.loop(0, 4)(combine)
 
     pl.when(lead & (z >= 1))(lambda: up_copy(0).wait_recv())
 
@@ -320,7 +320,18 @@
     pl.when(lead & (z + 2 < nz))(lambda: up_copy(1).start())
     pl.when(lead & (z >= 2))(lambda: tell(crest_2, z - 2))
 
-    pl.loop(6, chunks)(combine)
+    pl.loop(4, chunks - 1)(combine)
+
+    pl.when(lead & (z >= 2))(lambda: up_copy(1).wait_recv())
+
+    @pl.when(lead)
+    def _():
+        u2[...] = u1[...] + jnp.where(z >= 2, below[1], 0.0)
+
+    pl.when(lead & (z + 2 < nz))(lambda: pl.semaphore_wait(crest_2, 1))
+    pl.when(lead & (z + 4 < nz))(lambda: up_copy(2).start())
+
+    pl.loop(chunks - 1, chunks)(combine)
 
     def finish(c):
         for copy in copies_2(c):
@@ -334,18 +345,7 @@
             total = jnp.sum(values, axis=0, keepdims=True)
             wts_ref[:, pl.ds(pl.multiple_of(at + 128 * i, 128), 128)] = 2.5 * values / total
 
-    pl.loop(0, 3)(finish)
-
-    pl.when(lead & (z >= 2))(lambda: up_copy(1).wait_recv())
-
-    @pl.when(lead)
-    def _():
-        u2[...] = u1[...] + jnp.where(z >= 2, below[1], 0.0)
-
-    pl.when(lead & (z + 2 < nz))(lambda: pl.semaphore_wait(crest_2, 1))
-    pl.when(lead & (z + 4 < nz))(lambda: up_copy(2).start())
-
-    pl.loop(3, chunks)(finish)
+    pl.loop(0, 6)(finish)
 
     pl.when(lead & (z >= 4))(lambda: up_copy(2).wait_recv())
     when_upper(lambda r: down_copy(r).wait_recv())
@@ -357,6 +357,8 @@
             load = load + jnp.where(z + r + 1 < nz, above[r], 0.0)
         total[...] = load
         hand_over().start()
+
+    pl.loop(6, chunks)(finish)
 
     pl.when(core == 0)(lambda: hand_over().wait_recv())
     bias_copy_to(b1, br2, 1, cross).wait_recv()
@@ -437,7 +439,7 @@
             tile, tile, tile, tile, tile, tiles(group), tiles(line), tiles(3), tile, tile, tile, tile,
             dma((chunks,)), dma((3,)), dma((6, chunks)), dma((6, chunks)),
             dma((group,)), dma((group,)), dma((line,)), dma((line,)), dma((3,)), dma((3,)),
-            dma((2,)), dma((2,)), dma((2,)), *[pltpu.SemaphoreType.REGULAR] * 3,
+            dma((2,)), dma((2,)), dma((2,)), *[pltpu.SemaphoreType.REGULAR] * 2,
         ],
         compiler_params=pltpu.CompilerParams(
             collective_id=0, has_side_effects=True, vmem_limit_bytes=66300000

time: 21.7 us -> 20.4 us (0.940)
  Pallas kernels: 20.9 us -> 19.6 us
    pallas_call x1, Pallas kernels: 20.1 us -> 18.7 us  [local(): pl.pallas_call(functools.partial(kernel, sizes), out_shape=(pltpu.VMEM((o...]
where the time goes in v3:
time: 20.4 us; the launch traced here: 20.2 us
  Pallas kernels  19.6 us (96%)
  between operations  0.64 us (3%)
    pallas_call x1, Pallas kernels, local(): pl.pallas_call(functools.partial(kernel, sizes), out_shape=(pltpu.VMEM((o...  18.7 us
    pallas_call x1, Pallas kernels, local(): pl.pallas_call(hand_out, out_shape=tuple((jax.ShapeDtypeStruct(a.shape, a...  0.84 us

profile of v3, /device:TPU:1, one launch (start us, length us, event | category | flops | bytes accessed | tf_op | source)
XLA Modules:
  0.0 20.2 jit_solution(16499830409354483113)
XLA Ops:
  0.6 18.7 %router.1 = (f32[64,2048]{1,0:T(8,128)S(1)}, f32[8,2048]{1,0:T(8,128)S(1)}, f32[1,256]{1,0:T(1,128)S(1)}, f32[1,256]{1,0:T(1,128)S(1)}) custom-call(bf16[2048,1792]{1,0:T(8,128)(2,1)} %x_hbm.1, bf16[1792,256]{1,0:T(8,128)(2,1)} %w_hbm.1, s32[8,2048]{1,0:T(8,128)} %bitcast.6, f32[1,64]{1,0:T(1,128)} %bitcast.7), custom_call_target="tpu_custom_call" | custom-call | tf_op jit(solution)/shard_map/router/pallas_call | solution.py:419
  19.4 0.8 %hand_out.1 = (f32[64,2048]{1,0:T(8,128)}, f32[8,2048]{1,0:T(8,128)}, f32[1,256]{1,0:T(1,128)}, f32[1,256]{1,0:T(1,128)}) custom-call(f32[64,2048]{1,0:T(8,128)S(1)} %get-tuple-element.12.refs_0_, f32[8,2048]{1,0:T(8,128)S(1)} %get-tuple-element.13.refs_1_, f32[1,256]{1,0:T(1,128)S(1)} %get-tuple-element.14.refs_2_, f32[1,256]{1,0:T(1,128)S(1)} %get-tuple-element.15.refs_3_), custom_call_target="tpu_custom_call" | custom-call | tf_op jit(solution)/shard_map/hand_out/pallas_call | solution.py:449

commit v4 on v3

--- a/solution.py
+++ b/solution.py
@@ -37,9 +37,9 @@
 def kernel(
     sizes, x_hbm, w_hbm, ids_hbm, bias_hbm, aff_ref, wts_ref, load_ref, new_ref,
     x_v, w_v, wt_v, ids_v, bias_v, p_v, acc_v,
-    sa1, sb1, sa2, sb2, sc1, sc2, ra1, rb1, ra2, rb2, rc1, rc2,
+    sa1, sb1, sa2, sb2, sc1, sc2, r1, r2, rc1, rc2,
     hot_hi, hot_lo, d0, d1, u1, u2, total, near_by, above, below, b0, b1, br1, br2,
-    x_sem, in_sem, ss, rs, near_ss, near_rs, down_ss, down_rs, up_ss, up_rs, b_ss, b_rs, o_sem, crest_1, crest_2,
+    x_sem, in_sem, ss, rs1, rs2, rsc, near_sem, down_sem, up_ss, up_rs, b_ss, b_rs, o_sem, crest_1, crest_2,
 ):
     nz, nx, nc, chunks, width, target = sizes
     own = 64
@@ -160,14 +160,10 @@
             [code[:, 128 * i : 128 * (i + 1)] for i in range(width // 128)], axis=0
         ).astype(I16)
 
-    def remote(src, dst, c, kind, partner):
+    def remote(src, dst, send_sem, recv_sem, partner):
         return pltpu.make_async_remote_copy(
-            src_ref=src.at[c],
-            dst_ref=dst.at[c],
-            send_sem=ss.at[kind, c],
-            recv_sem=rs.at[kind, c],
-            device_id={"exp": partner},
-            device_id_type=MESH,
+            src_ref=src, dst_ref=dst, send_sem=send_sem, recv_sem=recv_sem,
+            device_id={"exp": partner}, device_id_type=MESH,
         )
 
     def even(c):
@@ -177,20 +173,28 @@
         return jnp.where(lax.rem(c, 2) == 0, cross, mate)
 
     def copies_ab(c):
-        return remote(sa1, ra1, c, 0, mate), remote(sb1, rb1, c, 1, cross)
+        return (
+            remote(sa1.at[c], r1.at[c, pl.ds(0, own)], ss.at[0], rs1.at[c], mate),
+            remote(sb1.at[c], r1.at[c, pl.ds(own, own)], ss.at[1], rs1.at[c], cross),
+        )
 
     def copy_c(c):
-        return remote(sc1, rc1, c, 2, even(c))
-
-    def copies_1(c):
-        return (*copies_ab(c), copy_c(c))
+        return remote(sc1.at[c], rc1.at[c], ss.at[2], rsc.at[0], even(c))
 
     def copies_2(c):
         return (
-            remote(sa2, ra2, c, 3, cross),
-            remote(sb2, rb2, c, 4, mate),
-            remote(sc2, rc2, c, 5, odd(c)),
-        )
+            remote(sa2.at[c], r2.at[c, pl.ds(0, half)], ss.at[3], rs2.at[c], cross),
+            remote(sb2.at[c], r2.at[c, pl.ds(half, half)], ss.at[4], rs2.at[c], mate),
+        )
+
+    def copy_c2(c):
+        return remote(sc2.at[c], rc2.at[c], ss.at[5], rsc.at[1], odd(c))
+
+    def arrived(dst, recv_sem):
+        remote(dst, dst, ss.at[0], recv_sem, mate).wait_recv()
+
+    def left(src, i):
+        remote(src, src, ss.at[i], rsc.at[0], mate).wait_send()
 
     def send(copies):
         for copy in copies:
@@ -204,19 +208,19 @@
 
     def count_copy(src, dst, r, sems, partner):
         return pltpu.make_async_remote_copy(
-            src_ref=src, dst_ref=dst.at[r], send_sem=sems[0].at[r], recv_sem=sems[1].at[r],
+            src_ref=src, dst_ref=dst.at[r], send_sem=sems[0], recv_sem=sems[1],
             device_id=partner, device_id_type=MESH,
         )
 
     def near_copy(r):
-        return count_copy(d0, near_by, r, (near_ss, near_rs), sibling(r))
+        return count_copy(d0, near_by, r, (near_sem.at[0], near_sem.at[1]), sibling(r))
 
     def down_copy(r):
-        return count_copy(d1, above, r, (down_ss, down_rs), {"tok_0": z - r - 1})
+        return count_copy(d1, above, r, (down_sem.at[0], down_sem.at[1]), {"tok_0": z - r - 1})
 
     def up_copy(i):
         src = (d1, u1, u2)[i]
-        return count_copy(src, below, i, (up_ss, up_rs), {"tok_0": z + (1, 2, 4)[i]})
+        return count_copy(src, below, i, (up_ss.at[i], up_rs.at[i]), {"tok_0": z + (1, 2, 4)[i]})
 
     def tell(sem, there):
         pl.semaphore_signal(sem, inc=1, device_id={"tok_0": there}, device_id_type=MESH)
@@ -225,9 +229,20 @@
         for r in range(nz - 1):
             pl.when(lead & (z > r))(functools.partial(action, r))
 
-    def when_upper(action):
-        for r in range(nz - 1):
-            pl.when(lead & (z + r + 1 < nz))(functools.partial(action, r))
+    def tiles_of(ref, n, sems):
+        return remote(ref.at[pl.ds(0, n)], ref.at[pl.ds(0, n)], sems.at[0], sems.at[1], mate)
+
+    def down_arrived():
+        for n in range(1, nz):
+            pl.when(lead & (z == nz - 1 - n))(
+                functools.partial(lambda n: tiles_of(above, n, down_sem).wait_recv(), n)
+            )
+
+    def down_left():
+        for n in range(1, nz):
+            pl.when(lead & (z == n))(
+                functools.partial(lambda n: tiles_of(above, n, down_sem).wait_send(), n)
+            )
 
     def near_sends(action):
         for r in range(len(siblings)):
@@ -280,8 +295,7 @@
 
     @pl.when(lead)
     def _():
-        for r in range(len(siblings)):
-            near_copy(r).wait_recv()
+        tiles_of(near_by, len(siblings), near_sem).wait_recv()
         d1[...] = sum((near_by[r] for r in range(len(siblings))), d0[...])
 
     when_lower(lambda r: down_copy(r).start())
@@ -294,18 +308,17 @@
     b1[...] = b0[...] + br1[...]
     bias_copy_to(b1, br2, 1, cross).start()
 
+    at_a = pl.ds(pl.multiple_of(pos_a * half, half), half)
+    off_a = pl.ds(pl.multiple_of((1 - pos_a) * half, half), half)
+    at_b = pl.ds(pl.multiple_of(own + pos_b * half, half), half)
+    off_b = pl.ds(pl.multiple_of(own + (1 - pos_b) * half, half), half)
+
     def combine(c):
-        for copy in copies_1(c):
-            copy.wait_recv()
-        at_a = pl.multiple_of(pos_a * half, half)
-        at_b = pl.multiple_of(pos_b * half, half)
-        off_a = pl.multiple_of((1 - pos_a) * half, half)
-        off_b = pl.multiple_of((1 - pos_b) * half, half)
-        sa2[c] = encode(part(c, cross, 0) + decode(ra1[c, pl.ds(off_a, half), :])).astype(I16)
-        sb2[c] = encode(part(c, mate, 1) + decode(rb1[c, pl.ds(off_b, half), :])).astype(I16)
-        sc2[c] = encode(decode(sc1[c]) + decode(rc1[c])).astype(I16)
-        acc_v[c, :half] = part(c, m, 0) + decode(ra1[c, pl.ds(at_a, half), :])
-        acc_v[c, half:] = part(c, m, 1) + decode(rb1[c, pl.ds(at_b, half), :])
+        arrived(r1.at[c], rs1.at[c])
+        sa2[c] = encode(part(c, cross, 0) + decode(r1[c, off_a, :])).astype(I16)
+        sb2[c] = encode(part(c, mate, 1) + decode(r1[c, off_b, :])).astype(I16)
+        acc_v[c, :half] = part(c, m, 0) + decode(r1[c, at_a, :])
+        acc_v[c, half:] = part(c, m, 1) + decode(r1[c, at_b, :])
         send(copies_2(c))
 
     pl.loop(0, 4)(combine)
@@ -320,7 +333,21 @@
     pl.when(lead & (z + 2 < nz))(lambda: up_copy(1).start())
     pl.when(lead & (z >= 2))(lambda: tell(crest_2, z - 2))
 
-    pl.loop(4, chunks - 1)(combine)
+    pl.loop(4, chunks)(combine)
+
+    arrived(rc1, rsc.at[0])
+    for c in range(chunks):
+        sc2[c] = encode(decode(sc1[c]) + decode(rc1[c])).astype(I16)
+    for c in range(chunks):
+        copy_c2(c).start()
+
+    def finish(c):
+        arrived(r2.at[c], rs2.at[c])
+        at = pl.ds(pl.multiple_of(c * width, width), width)
+        aff_ref[:half, at] = sigmoid(acc_v[c, :half] + decode(r2[c, :half]))
+        aff_ref[half:, at] = sigmoid(acc_v[c, half:] + decode(r2[c, half:]))
+
+    pl.loop(0, 2)(finish)
 
     pl.when(lead & (z >= 2))(lambda: up_copy(1).wait_recv())
 
@@ -331,24 +358,10 @@
     pl.when(lead & (z + 2 < nz))(lambda: pl.semaphore_wait(crest_2, 1))
     pl.when(lead & (z + 4 < nz))(lambda: up_copy(2).start())
 
-    pl.loop(chunks - 1, chunks)(combine)
-
-    def finish(c):
-        for copy in copies_2(c):
-            copy.wait_recv()
-        at = pl.multiple_of(c * width, width)
-        aff_ref[:half, pl.ds(at, width)] = sigmoid(acc_v[c, :half] + decode(ra2[c]))
-        aff_ref[half:, pl.ds(at, width)] = sigmoid(acc_v[c, half:] + decode(rb2[c]))
-        chosen = sigmoid(decode(sc2[c]) + decode(rc2[c]))
-        for i in range(width // 128):
-            values = chosen[8 * i : 8 * i + 8]
-            total = jnp.sum(values, axis=0, keepdims=True)
-            wts_ref[:, pl.ds(pl.multiple_of(at + 128 * i, 128), 128)] = 2.5 * values / total
-
-    pl.loop(0, 6)(finish)
+    pl.loop(2, 6)(finish)
 
     pl.when(lead & (z >= 4))(lambda: up_copy(2).wait_recv())
-    when_upper(lambda r: down_copy(r).wait_recv())
+    down_arrived()
 
     @pl.when(lead)
     def _():
@@ -359,6 +372,14 @@
         hand_over().start()
 
     pl.loop(6, chunks)(finish)
+
+    arrived(rc2, rsc.at[1])
+    for c in range(chunks):
+        chosen = sigmoid(decode(sc2[c]) + decode(rc2[c]))
+        for i in range(width // 128):
+            values = chosen[8 * i : 8 * i + 8]
+            at = pl.ds(c * width + 128 * i, 128)
+            wts_ref[:, at] = 2.5 * values / jnp.sum(values, axis=0, keepdims=True)
 
     pl.when(core == 0)(lambda: hand_over().wait_recv())
     bias_copy_to(b1, br2, 1, cross).wait_recv()
@@ -370,14 +391,13 @@
         load_ref[:, 128 * i : 128 * (i + 1)] = load[i : i + 1]
         new_ref[:, 128 * i : 128 * (i + 1)] = new_bias[i : i + 1]
 
-    @pl.loop(0, chunks)
-    def _(c):
-        for copy in (*copies_1(c), *copies_2(c)):
-            copy.wait_send()
-
-    near_sends(lambda r: near_copy(r).wait_send())
+    for i, src in enumerate((sa1, sb1, sc1, sa2, sb2, sc2)):
+        left(src, i)
+    pl.when(core == 0)(lambda: tiles_of(near_by, nx, near_sem).wait_send())
+    if nx > 1:
+        pl.when(lead)(lambda: tiles_of(near_by, nx - 1, near_sem).wait_send())
     pl.when(lead)(lambda: hand_over().wait_send())
-    when_lower(lambda r: down_copy(r).wait_send())
+    down_left()
     pl.when(lead & (z + 1 < nz))(lambda: up_copy(0).wait_send())
     pl.when(lead & (z + 2 < nz))(lambda: up_copy(1).wait_send())
     pl.when(lead & (z + 4 < nz))(lambda: up_copy(2).wait_send())
@@ -434,11 +454,12 @@
             pltpu.VMEM((1, own), F32),
             pltpu.VMEM((chunks, experts, width), F32),
             pltpu.VMEM((chunks, own, width), F32),
-            big, big, small, small, few, few, big, big, small, small, few, few,
+            big, big, small, small, few, few,
+            pltpu.VMEM((chunks, 2 * own, width), I16), pltpu.VMEM((chunks, own, width), I16), few, few,
             pltpu.VMEM((128, rows), BF16), pltpu.VMEM((128, rows), BF16),
             tile, tile, tile, tile, tile, tiles(group), tiles(line), tiles(3), tile, tile, tile, tile,
-            dma((chunks,)), dma((3,)), dma((6, chunks)), dma((6, chunks)),
-            dma((group,)), dma((group,)), dma((line,)), dma((line,)), dma((3,)), dma((3,)),
+            dma((chunks,)), dma((3,)), dma((6,)), dma((chunks,)), dma((chunks,)), dma((2,)),
+            dma((2,)), dma((2,)), dma((3,)), dma((3,)),
             dma((2,)), dma((2,)), dma((2,)), *[pltpu.SemaphoreType.REGULAR] * 2,
         ],
         compiler_params=pltpu.CompilerParams(

time: 20.4 us -> 19.5 us (0.956)
  Pallas kernels: 19.6 us -> 18.7 us
    pallas_call x1, Pallas kernels: 18.7 us -> 17.9 us  [local(): pl.pallas_call(functools.partial(kernel, sizes), out_shape=(pltpu.VMEM((o...]
where the time goes in v4:
time: 19.5 us; the launch traced here: 19.3 us
  Pallas kernels  18.7 us (96%)
  between operations  0.64 us (3%)
    pallas_call x1, Pallas kernels, local(): pl.pallas_call(functools.partial(kernel, sizes), out_shape=(pltpu.VMEM((o...  17.9 us
    pallas_call x1, Pallas kernels, local(): pl.pallas_call(hand_out, out_shape=tuple((jax.ShapeDtypeStruct(a.shape, a...  0.84 us

profile of v4, /device:TPU:1, one launch (start us, length us, event | category | flops | bytes accessed | tf_op | source)
XLA Modules:
  0.0 19.3 jit_solution(5855278170920282585)
XLA Ops:
  0.6 17.9 %router.1 = (f32[64,2048]{1,0:T(8,128)S(1)}, f32[8,2048]{1,0:T(8,128)S(1)}, f32[1,256]{1,0:T(1,128)S(1)}, f32[1,256]{1,0:T(1,128)S(1)}) custom-call(bf16[2048,1792]{1,0:T(8,128)(2,1)} %x_hbm.1, bf16[1792,256]{1,0:T(8,128)(2,1)} %w_hbm.1, s32[8,2048]{1,0:T(8,128)} %bitcast.6, f32[1,64]{1,0:T(1,128)} %bitcast.7), custom_call_target="tpu_custom_call" | custom-call | tf_op jit(solution)/shard_map/router/pallas_call | solution.py:439
  18.5 0.8 %hand_out.1 = (f32[64,2048]{1,0:T(8,128)}, f32[8,2048]{1,0:T(8,128)}, f32[1,256]{1,0:T(1,128)}, f32[1,256]{1,0:T(1,128)}) custom-call(f32[64,2048]{1,0:T(8,128)S(1)} %get-tuple-element.12.refs_0_, f32[8,2048]{1,0:T(8,128)S(1)} %get-tuple-element.13.refs_1_, f32[1,256]{1,0:T(1,128)S(1)} %get-tuple-element.14.refs_2_, f32[1,256]{1,0:T(1,128)S(1)} %get-tuple-element.15.refs_3_), custom_call_target="tpu_custom_call" | custom-call | tf_op jit(solution)/shard_map/hand_out/pallas_call | solution.py:470

commit v5 on v4

--- a/solution.py
+++ b/solution.py
@@ -128,6 +128,7 @@
 
     w_copy.wait()
     x_copy(1).start()
+    x_copy(2).start()
     wt_v[...] = w_v[...].T
 
     low_a = jnp.where((m == 0) | (m == 3), 1, 0)
@@ -260,38 +261,30 @@
             device_id={"exp": partner}, device_id_type=MESH,
         )
 
-    x_copy(0).wait()
-    x_copy(2).start()
-    compute(0)
-    pl.semaphore_wait(barrier, greeted)
-    send(copies_ab(0))
-    near_sends(lambda r: near_copy(r).start())
-    x_copy(3).start()
-    choose(0)
-    copy_c(0).start()
-
-    bias_copy.wait()
-    mine = bias_v[...]
-    mine = jnp.broadcast_to(jnp.concatenate([mine, mine], axis=1), (8, 128))
-    my_row = jnp.where(m < 2, 0, 1)
-    b0[...] = jnp.where((sub == my_row) & ((lane >> 6) == pos_b), mine, 0.0)
-
-
-    x_copy(1).wait()
-    x_copy(4).start()
-    stage_1(1)
-    bias_copy_to(b0, br1, 0, mate).start()
-
-    def later(c):
+    @pl.loop(0, chunks)
+    def _(c):
         x_copy(c).wait()
 
         @pl.when(c + 3 < chunks)
         def _():
             x_copy(c + 3).start()
 
-        stage_1(c)
-
-    pl.loop(2, chunks - 1)(later)
+        compute(c)
+        pl.when(c == 0)(lambda: pl.semaphore_wait(barrier, greeted))
+        send(copies_ab(c))
+
+        @pl.when(c == 0)
+        def _():
+            near_sends(lambda r: near_copy(r).start())
+            bias_copy.wait()
+            mine = bias_v[...]
+            mine = jnp.broadcast_to(jnp.concatenate([mine, mine], axis=1), (8, 128))
+            my_row = jnp.where(m < 2, 0, 1)
+            b0[...] = jnp.where((sub == my_row) & ((lane >> 6) == pos_b), mine, 0.0)
+            bias_copy_to(b0, br1, 0, mate).start()
+
+        choose(c)
+        copy_c(c).start()
 
     @pl.when(lead)
     def _():
@@ -301,8 +294,6 @@
     when_lower(lambda r: down_copy(r).start())
     pl.when(lead & (z + 1 < nz))(lambda: up_copy(0).start())
     pl.when(lead & (z >= 1))(lambda: tell(crest_1, z - 1))
-
-    pl.loop(chunks - 1, chunks)(later)
 
     bias_copy_to(b0, br1, 0, mate).wait_recv()
     b1[...] = b0[...] + br1[...]
@@ -321,19 +312,21 @@
         acc_v[c, half:] = part(c, m, 1) + decode(r1[c, at_b, :])
         send(copies_2(c))
 
-    pl.loop(0, 4)(combine)
-
-    pl.when(lead & (z >= 1))(lambda: up_copy(0).wait_recv())
-
-    @pl.when(lead)
-    def _():
-        u1[...] = d1[...] + jnp.where(z >= 1, below[0], 0.0)
-
-    pl.when(lead & (z + 1 < nz))(lambda: pl.semaphore_wait(crest_1, 1))
-    pl.when(lead & (z + 2 < nz))(lambda: up_copy(1).start())
-    pl.when(lead & (z >= 2))(lambda: tell(crest_2, z - 2))
-
-    pl.loop(4, chunks)(combine)
+    def second_step():
+        pl.when(lead & (z >= 1))(lambda: up_copy(0).wait_recv())
+
+        @pl.when(lead)
+        def _():
+            u1[...] = d1[...] + jnp.where(z >= 1, below[0], 0.0)
+
+        pl.when(lead & (z + 1 < nz))(lambda: pl.semaphore_wait(crest_1, 1))
+        pl.when(lead & (z + 2 < nz))(lambda: up_copy(1).start())
+        pl.when(lead & (z >= 2))(lambda: tell(crest_2, z - 2))
+
+    @pl.loop(0, chunks)
+    def _(c):
+        combine(c)
+        pl.when(c == 3)(second_step)
 
     arrived(rc1, rsc.at[0])
     for c in range(chunks):
@@ -347,31 +340,33 @@
         aff_ref[:half, at] = sigmoid(acc_v[c, :half] + decode(r2[c, :half]))
         aff_ref[half:, at] = sigmoid(acc_v[c, half:] + decode(r2[c, half:]))
 
-    pl.loop(0, 2)(finish)
-
-    pl.when(lead & (z >= 2))(lambda: up_copy(1).wait_recv())
-
-    @pl.when(lead)
-    def _():
-        u2[...] = u1[...] + jnp.where(z >= 2, below[1], 0.0)
-
-    pl.when(lead & (z + 2 < nz))(lambda: pl.semaphore_wait(crest_2, 1))
-    pl.when(lead & (z + 4 < nz))(lambda: up_copy(2).start())
-
-    pl.loop(2, 6)(finish)
-
-    pl.when(lead & (z >= 4))(lambda: up_copy(2).wait_recv())
-    down_arrived()
-
-    @pl.when(lead)
-    def _():
-        load = u2[...] + jnp.where(z >= 4, below[2], 0.0)
-        for r in range(nz - 1):
-            load = load + jnp.where(z + r + 1 < nz, above[r], 0.0)
-        total[...] = load
-        hand_over().start()
-
-    pl.loop(6, chunks)(finish)
+    def third_step():
+        pl.when(lead & (z >= 2))(lambda: up_copy(1).wait_recv())
+
+        @pl.when(lead)
+        def _():
+            u2[...] = u1[...] + jnp.where(z >= 2, below[1], 0.0)
+
+        pl.when(lead & (z + 2 < nz))(lambda: pl.semaphore_wait(crest_2, 1))
+        pl.when(lead & (z + 4 < nz))(lambda: up_copy(2).start())
+
+    def sum_up():
+        pl.when(lead & (z >= 4))(lambda: up_copy(2).wait_recv())
+        down_arrived()
+
+        @pl.when(lead)
+        def _():
+            load = u2[...] + jnp.where(z >= 4, below[2], 0.0)
+            for r in range(nz - 1):
+                load = load + jnp.where(z + r + 1 < nz, above[r], 0.0)
+            total[...] = load
+            hand_over().start()
+
+    @pl.loop(0, chunks)
+    def _(c):
+        finish(c)
+        pl.when(c == 0)(third_step)
+        pl.when(c == chunks - 1)(sum_up)
 
     arrived(rc2, rsc.at[1])
     for c in range(chunks):

time: 19.5 us -> 19.5 us (level)
  no operation moved by 1% of the time
where the time goes in v5:
time: 19.5 us; the launch traced here: 19.4 us
  Pallas kernels  18.8 us (96%)
  between operations  0.64 us (3%)
    pallas_call x1, Pallas kernels, local(): pl.pallas_call(functools.partial(kernel, sizes), out_shape=(pltpu.VMEM((o...  17.9 us
    pallas_call x1, Pallas kernels, local(): pl.pallas_call(hand_out, out_shape=tuple((jax.ShapeDtypeStruct(a.shape, a...  0.84 us

profile of v5, /device:TPU:1, one launch (start us, length us, event | category | flops | bytes accessed | tf_op | source)
XLA Modules:
  0.0 19.4 jit_solution(15667660028867795896)
XLA Ops:
  0.6 17.9 %router.1 = (f32[64,2048]{1,0:T(8,128)S(1)}, f32[8,2048]{1,0:T(8,128)S(1)}, f32[1,256]{1,0:T(1,128)S(1)}, f32[1,256]{1,0:T(1,128)S(1)}) custom-call(bf16[2048,1792]{1,0:T(8,128)(2,1)} %x_hbm.1, bf16[1792,256]{1,0:T(8,128)(2,1)} %w_hbm.1, s32[8,2048]{1,0:T(8,128)} %bitcast.6, f32[1,64]{1,0:T(1,128)} %bitcast.7), custom_call_target="tpu_custom_call" | custom-call | tf_op jit(solution)/shard_map/router/pallas_call | solution.py:434
  18.6 0.8 %hand_out.1 = (f32[64,2048]{1,0:T(8,128)}, f32[8,2048]{1,0:T(8,128)}, f32[1,256]{1,0:T(1,128)}, f32[1,256]{1,0:T(1,128)}) custom-call(f32[64,2048]{1,0:T(8,128)S(1)} %get-tuple-element.12.refs_0_, f32[8,2048]{1,0:T(8,128)S(1)} %get-tuple-element.13.refs_1_, f32[1,256]{1,0:T(1,128)S(1)} %get-tuple-element.14.refs_2_, f32[1,256]{1,0:T(1,128)S(1)} %get-tuple-element.15.refs_3_), custom_call_target="tpu_custom_call" | custom-call | tf_op jit(solution)/shard_map/hand_out/pallas_call | solution.py:465
